TPU v7x, 32 devices: a whole 2x2x4 slice. The times are simulated.
32 devices in a mesh: ta: 4 (over y, x), gz: 2 (over core), xy: 4 (over z).
Axes of the slice: x: 2, y: 2, z: 4, core: 2. Of those that a mesh axis runs over, the one named last changes fastest.
Arguments:
- source_field: float32 [2, 4, 3, 4, 2, 4, 128], P(None, None, None, 'ta', 'gz', 'xy'), may hold values from -6 to 6
- gauge_links: float32 [2, 8, 3, 3, 4, 2, 4, 128], P(None, None, None, None, 'ta', 'gz', 'xy'), may hold values from -2.5 to 2.5
- fine_vectors: bfloat16 [2, 24, 4, 3, 4, 2, 4, 128], P(None, None, None, None, 'ta', 'gz', 'xy'), may hold values from -1.75 to 1.75
- middle_blocks: float32 [2, 9, 24, 4, 2, 4, 768], P(None, None, None, 'ta', 'gz', 'xy'), may hold values from -0.3125 to 0.3125
- middle_vectors: float32 [2, 24, 4, 2, 4, 768], P(None, None, 'ta', 'gz', 'xy'), may hold values from -0.625 to 0.625
- bottom_blocks: float32 [2, 7, 4, 2, 2304], P(None, None, 'ta', 'gz'), may hold values from -4 to 4
Outputs:
- solution: float32 [2, 4, 3, 4, 2, 4, 128], P(None, None, None, 'ta', 'gz', 'xy')
- smoothed_residual: float32 [2, 4, 3, 4, 2, 4, 128], P(None, None, None, 'ta', 'gz', 'xy')
All inputs are finite; a program needn't handle non-finite values.
Results may differ from a plain program's by a relative error of at most 0.0034.
Values sent between devices are 32-bit elements; how exact they have to be, the bound alone decides.
A program may use at most 64 MiB of HBM per device.

v0:
```python
import functools

import jax
import jax.numpy as jnp
from jax import lax
from jax.experimental import pallas as pl
from jax.experimental.pallas import tpu as pltpu
from jax.sharding import PartitionSpec as P

BY = 4
NV = 24
NC = 3
NSC = 12

DIAGONAL = 4.0 + 0.1
TWIST = 0.1
DENOMINATOR = DIAGONAL * DIAGONAL + TWIST * TWIST
FINE_DAMPING = 0.8
MIDDLE_DAMPING = 0.4
MIDDLE_SHIFT = 2.0
BOTTOM_SHIFT = 2.0
MESH = pl.DeviceIdType.MESH
F32 = jnp.float32
BF16 = jnp.bfloat16
AXES = ("ta", "gz", "xy")


def plan(sizes):
    n_ta, n_gz, n_xy = sizes
    lines = []
    for offset in ((0, 0), (1, 0), (-1, 0), (0, 1), (0, -1)):
        reduced = (offset[0] % n_ta, offset[1] % n_gz)
        if reduced not in lines:
            lines.append(reduced)
    hops = []
    for axis in range(3):
        for step in (1, -1):
            offset = [0, 0, 0]
            offset[axis] = -step % sizes[axis]
            hops.append(tuple(offset))
    plane = [(a, b) for a in range(n_ta) for b in range(n_gz) if (a, b) != (0, 0)]
    spread = [(a, b, x) for a, b in lines for x in range(n_xy) if (a, b, x) != (0, 0, 0)]
    peers = []
    for offset in hops + [(a, b, 0) for a, b in plane] + spread:
        back = tuple(-o % n for o, n in zip(offset, sizes))
        for one in (offset, back):
            if one not in peers:
                peers.append(one)
    return lines, hops, plane, spread, peers


def dot(a, b, dims=((1,), (0,))):
    return lax.dot_general(
        a, b, (dims, ((), ())), precision=lax.Precision.HIGHEST, preferred_element_type=F32
    )


def split_dot(a, b, dims):
    high = a.astype(BF16)
    low = (a - high.astype(F32)).astype(BF16)
    rows = a.shape[0]
    both = lax.dot_general(
        jnp.concatenate([high, low], axis=0), b, (dims, ((), ())), preferred_element_type=F32
    )
    return both[:rows] + both[rows:]


def iota(shape, dim):
    return lax.broadcasted_iota(jnp.int32, shape, dim)


def hopping(load, gauge):
    row = iota((8, 128), 0)
    odd = (row & 1) == 1
    m = row >> 1
    near = m < 2
    eps = jnp.where(odd, 1.0, -1.0).astype(F32)

    def phase(values):
        re = jnp.zeros((8, 128), F32)
        im = jnp.zeros((8, 128), F32)
        for i, (a, b) in enumerate(values):
            re = jnp.where(m == i, a, re)
            im = jnp.where(m == i, b, im)
        return re * eps, im * eps

    up0 = phase(((1.0, 0.0), (0.0, 1.0), (0.0, 1.0), (-1.0, 0.0)))
    up1 = phase(((1.0, 0.0), (0.0, -1.0), (0.0, 1.0), (1.0, 0.0)))
    low2 = phase(((1.0, 0.0), (0.0, -1.0), (0.0, -1.0), (1.0, 0.0)))
    low3 = phase(((1.0, 0.0), (0.0, 1.0), (0.0, -1.0), (-1.0, 0.0)))

    def times(c, re, im):
        return c[0] * re - c[1] * im, c[0] * im + c[1] * re

    half = {}
    for color in range(NC):
        v = [load(spin, color) for spin in range(4)]
        for spin, c in ((0, up0), (1, up1)):
            first, other = (v[2], v[3]) if spin == 0 else (v[3], v[2])
            re = jnp.where(near, first[0], other[0])
            im = jnp.where(near, first[1], other[1])
            re, im = times(c, re, im)
            half[spin, color] = (v[spin][0] + re, v[spin][1] + im)
    out = {}
    for c in range(NC):
        acc = {0: None, 1: None}
        for k in range(NC):
            ure = gauge[pl.ds(c * 3 + k, 8, stride=9), :]
            uim = gauge[pl.ds(72 + c * 3 + k, 8, stride=9), :]
            for spin in range(2):
                hre, him = half[spin, k]
                re = ure * hre - uim * him
                im = ure * him + uim * hre
                acc[spin] = (re, im) if acc[spin] is None else (acc[spin][0] + re, acc[spin][1] + im)
        w0, w1 = acc[0], acc[1]
        out[0, c] = w0
        out[1, c] = w1
        for spin, coef in ((2, low2), (3, low3)):
            first, other = (w0, w1) if spin == 2 else (w1, w0)
            re = jnp.where(near, first[0], other[0])
            im = jnp.where(near, first[1], other[1])
            out[spin, c] = times(coef, re, im)
    rows = [
        jnp.sum(out[spin, c][part], axis=0, keepdims=True)
        for part in range(2)
        for spin in range(4)
        for c in range(NC)
    ]
    return jnp.concatenate(rows, axis=0)


def signs_of():
    row = iota((24, 128), 0)
    inner = jnp.where(row >= NSC, row - NSC, row)
    return jnp.where(inner < 6, 1.0, -1.0).astype(F32), row < NSC


def swap(v):
    return jnp.concatenate([v[NSC:], v[:NSC]], axis=0)


def twisted(v):
    g5, real = signs_of()
    return DIAGONAL * v + TWIST * jnp.where(real, -g5, g5) * swap(v)


def precondition(v):
    g5, real = signs_of()
    return (DIAGONAL * v + TWIST * jnp.where(real, g5, -g5) * swap(v)) * (1.0 / DENOMINATOR)


def kernel(
    sizes, source, gauge_hbm, fine, mb_hbm, mv_hbm, bb_hbm,
    solution_ref, residual_ref,
    gauge, mb, mv, bb, fine32, near1, near2, second, expand, reduce,
    rsend, rbuf, fsend, fbuf, psend, pbuf, tsend, tbuf,
    local_sem, send_sem, recv_sem,
):
    n_ta, n_gz, n_xy = sizes
    lines, hops, plane, spread, peers = plan(sizes)
    me = tuple(lax.axis_index(a) for a in AXES)
    chunks = n_xy * NV * NV // 128
    width = rsend.shape[1]

    def device(offset):
        return tuple(lax.rem(m + o, n) for m, o, n in zip(me, offset, sizes))

    loads = [
        pltpu.make_async_copy(gauge_hbm, gauge, local_sem.at[0]),
        pltpu.make_async_copy(mb_hbm, mb, local_sem.at[1]),
        pltpu.make_async_copy(mv_hbm, mv, local_sem.at[2]),
        pltpu.make_async_copy(bb_hbm, bb.at[pl.ds(0, 14 * chunks)], local_sem.at[3]),
    ]
    barrier = pltpu.get_barrier_semaphore()
    for offset in peers:
        pl.semaphore_signal(barrier, inc=1, device_id=device(offset), device_id_type=MESH)
    for load in loads:
        load.start()

    bb[pl.ds(14 * chunks, bb.shape[0] - 14 * chunks), :] = jnp.zeros(
        (bb.shape[0] - 14 * chunks, 128), F32
    )
    count = [0]

    def send(src, dst, offset):
        copy = pltpu.make_async_remote_copy(
            src_ref=src, dst_ref=dst, send_sem=send_sem.at[count[0]],
            recv_sem=recv_sem.at[count[0]], device_id=device(offset), device_id_type=MESH,
        )
        count[0] += 1
        copy.start()
        return copy

    pl.semaphore_wait(barrier, len(peers))
    pending = []

    def halo(src, buf):
        return [send(src, buf.at[pl.ds(24 * i, 24)], offset) for i, offset in enumerate(hops)]

    def fill_y(v, buf):
        buf[pl.ds(24 * 6, 24), :] = pltpu.roll(v, 127, 1)
        buf[pl.ds(24 * 7, 24), :] = pltpu.roll(v, 1, 1)

    copies1 = halo(source, near1)
    pending += copies1
    src = source[...]
    fill_y(src, near1)
    first = FINE_DAMPING * precondition(src)

    cols = n_xy * NV * NV
    n = iota((1, cols), 1).astype(F32)
    xs = jnp.floor((n + 0.5) * (1.0 / (NV * NV)))
    js = jnp.floor((n - xs * (NV * NV) + 0.5) * (1.0 / NV))
    ks = n - xs * (NV * NV) - js * NV
    lane = iota((width, cols), 0).astype(F32)
    expand[...] = jnp.where(lane == xs * NV + ks, 1.0, 0.0).astype(BF16)
    reduce[...] = jnp.where(lane == xs * NV + js, 1.0, 0.0).astype(BF16)
    fine32[...] = fine[...].astype(F32)

    def loader(buf, scaled):
        def load(spin, color):
            i = spin * NC + color
            re = buf[pl.ds(i, 8, stride=24), :]
            im = buf[pl.ds(NSC + i, 8, stride=24), :]
            if not scaled:
                return re, im
            a = FINE_DAMPING * DIAGONAL / DENOMINATOR
            b = FINE_DAMPING * TWIST / DENOMINATOR * (1.0 if spin < 2 else -1.0)
            return a * re + b * im, a * im - b * re
        return load

    loads[0].wait()
    for copy in copies1:
        copy.wait_recv()
    hop = hopping(loader(near1, True), gauge)
    second_value = first + FINE_DAMPING * precondition(src - (twisted(first) - 0.5 * hop))
    second[...] = second_value
    copies2 = halo(second, near2)
    pending += copies2
    fill_y(second_value, near2)
    loads[2].wait()
    loads[3].wait()
    loads[1].wait()
    for copy in copies2:
        copy.wait_recv()
    hop = hopping(loader(near2, False), gauge)
    smoothed = src - (twisted(second_value) - 0.5 * hop)
    residual_ref[...] = smoothed
    low = smoothed.astype(BF16).astype(F32)

    mre = jnp.zeros((NV, 128), F32)
    mim = jnp.zeros((NV, 128), F32)
    for i in range(NSC):
        fre = fine32[pl.ds(i, NV, stride=NSC), :]
        fim = fine32[pl.ds(NV * NSC + i, NV, stride=NSC), :]
        rre, rim = low[i : i + 1], low[NSC + i : NSC + i + 1]
        mre = mre + fre * rre + fim * rim
        mim = mim + fre * rim - fim * rre
    sums = jnp.concatenate([mre, mim], axis=0)
    li = iota((128, 128), 0)
    lj = iota((128, 128), 1)
    group = jnp.where((li >> 2) == (lj & 31), 1.0, 0.0).astype(F32)
    rep = dot(sums, group)
    own_group = ((iota((48, 128), 0) & 3) == (iota((48, 128), 1) >> 5))
    masked = jnp.where(own_group, rep, 0.0)
    gather = jnp.where(iota((16, 48), 0) == (iota((16, 48), 1) >> 2), 1.0, 0.0).astype(F32)
    mr = dot(gather, masked)

    are = jnp.zeros((NV, 128), F32)
    aim = jnp.zeros((NV, 128), F32)
    for c in range(6):
        vre = mv[pl.ds(c, NV, stride=6), :]
        vim = mv[pl.ds(NV * 6 + c, NV, stride=6), :]
        rre, rim = mr[c : c + 1], mr[6 + c : 7 + c]
        are = are + vre * rre + vim * rim
        aim = aim + vre * rim - vim * rre
    rcol_re = jnp.sum(are, axis=1, keepdims=True)
    rcol_im = jnp.sum(aim, axis=1, keepdims=True)
    place = iota((NV, width), 1) == me[2] * NV + iota((NV, width), 0)
    own_re = jnp.sum(jnp.where(place, rcol_re, 0.0), axis=0, keepdims=True)
    own_im = jnp.sum(jnp.where(place, rcol_im, 0.0), axis=0, keepdims=True)
    tile_row = iota((8, width), 0)

    def pair_tile(re, im):
        return jnp.where(tile_row == 0, re, jnp.where(tile_row == 1, im, 0.0))

    own_tile = pair_tile(own_re, own_im)
    rsend[...] = own_tile
    copies3 = []
    for a, b, x in spread:
        slot = lines.index((-a % n_ta, -b % n_gz))
        copies3.append(send(rsend, rbuf.at[slot * n_xy + x], (a, b, x)))
    pending += copies3

    def prolong(re, im):
        re = jnp.broadcast_to(re, (NV, 128))
        im = jnp.broadcast_to(im, (NV, 128))
        rows_re, rows_im = [], []
        for c in range(6):
            vre = mv[pl.ds(c, NV, stride=6), :]
            vim = mv[pl.ds(NV * 6 + c, NV, stride=6), :]
            rows_re.append(jnp.sum(vre * re - vim * im, axis=0, keepdims=True))
            rows_im.append(jnp.sum(vre * im + vim * re, axis=0, keepdims=True))
        zero = jnp.zeros((2, 128), F32)
        return jnp.concatenate(rows_re + [zero] + rows_im + [zero], axis=0)

    psend[pl.ds(0, 16), :] = prolong(rcol_re, rcol_im)

    for copy in copies3:
        copy.wait_recv()

    def line_slot(offset):
        return lines.index((offset[0] % n_ta, offset[1] % n_gz))

    near_offsets = ((1, 0), (-1, 0), (0, 1), (0, -1))
    length = n_xy * NV

    def turn(v, shift):
        lanes = iota(v.shape, 1)
        if shift > 0:
            inside, wrapped = lanes < length - shift, length - shift
            one, two = pltpu.roll(v, width - shift, 1), pltpu.roll(v, wrapped, 1)
        else:
            inside = lanes >= -shift
            one, two = pltpu.roll(v, -shift, 1), pltpu.roll(v, width - (length + shift), 1)
        return jnp.where(lanes < length, jnp.where(inside, one, two), 0.0)

    def bottom(own, others):
        near = [own] + others + [turn(own, NV), turn(own, -NV)]
        zero = jnp.zeros((1, width), F32)
        stack = jnp.concatenate(
            [v[0:1] for v in near] + [zero] + [v[1:2] for v in near] + [zero], axis=0
        )
        wide = split_dot(stack, expand[...], ((1,), (0,)))
        parts = []
        for c in range(chunks):
            bre = bb[pl.ds(c, 8, stride=chunks), :]
            bim = bb[pl.ds(7 * chunks + c, 8, stride=chunks), :]
            vre = wide[0:8, c * 128 : (c + 1) * 128]
            vim = wide[8:16, c * 128 : (c + 1) * 128]
            parts.append(jnp.concatenate([bre * vre - bim * vim, bre * vim + bim * vre], axis=0))
        prod = jnp.concatenate(parts, axis=1)
        short = split_dot(prod, reduce[...], ((1,), (1,)))
        re = jnp.sum(short[0:8], axis=0, keepdims=True)
        im = jnp.sum(short[8:16], axis=0, keepdims=True)
        return pair_tile(re, im) + BOTTOM_SHIFT * own

    def gathered(slot):
        total = own_tile if slot == 0 else rbuf[slot * n_xy]
        for x in range(1, n_xy):
            total = total + rbuf[slot * n_xy + x]
        return total

    slots = [gathered(s) for s in range(len(lines))]
    r = slots[0]
    f = bottom(r, [slots[line_slot(o)] for o in near_offsets])
    fsend[...] = f
    copies4 = []
    for i, (a, b) in enumerate(lines):
        if i:
            copies4.append(send(fsend, fbuf.at[lines.index((-a % n_ta, -b % n_gz))], (a, b, 0)))
    pending += copies4
    fcol_re = jnp.sum(jnp.where(place, f[0:1], 0.0), axis=1, keepdims=True)
    fcol_im = jnp.sum(jnp.where(place, f[1:2], 0.0), axis=1, keepdims=True)
    psend[pl.ds(16, 16), :] = prolong(fcol_re, fcol_im)
    copies5 = [send(psend, pbuf.at[pl.ds(32 * i, 32)], offset) for i, offset in enumerate(hops)]
    pending += copies5
    for copy in copies4:
        copy.wait_recv()
    s = bottom(f, [fbuf[line_slot(o)] for o in near_offsets])

    rr, ri, fr, fi, sr, si = r[0:1], r[1:2], f[0:1], f[1:2], s[0:1], s[1:2]
    tsend[...] = jnp.concatenate(
        [
            fr * fr + fi * fi,
            sr * sr + si * si,
            fr * sr + fi * si,
            fr * si - fi * sr,
            fr * rr + fi * ri,
            fr * ri - fi * rr,
            sr * rr + si * ri,
            sr * ri - si * rr,
        ],
        axis=0,
    )
    copies6 = []
    for i, (a, b) in enumerate(plane):
        copies6.append(send(tsend, tbuf.at[i], (a, b, 0)))
    pending += copies6

    own_p = psend[...]
    lane32 = iota((32, 128), 1) & 31
    y_up = jnp.where(lane32 == 31, pltpu.roll(own_p, 31, 1), pltpu.roll(own_p, 127, 1))
    y_down = jnp.where(lane32 == 0, pltpu.roll(own_p, 97, 1), pltpu.roll(own_p, 1, 1))
    acc = [jnp.zeros((NV, 128), F32) for _ in range(4)]

    def add_direction(acc, d, v):
        acc = list(acc)
        for c in range(6):
            bre = mb[pl.ds(d * NV * 6 + c, NV, stride=6), :]
            bim = mb[pl.ds((9 + d) * NV * 6 + c, NV, stride=6), :]
            for image in range(2):
                vre = v[16 * image + c : 16 * image + c + 1]
                vim = v[16 * image + 8 + c : 16 * image + 9 + c]
                acc[2 * image] = acc[2 * image] + bre * vre - bim * vim
                acc[2 * image + 1] = acc[2 * image + 1] + bre * vim + bim * vre
        return acc

    acc = add_direction(acc, 0, own_p)
    acc = add_direction(acc, 7, y_up)
    acc = add_direction(acc, 8, y_down)
    for copy in copies5:
        copy.wait_recv()
    for i in range(6):
        acc = add_direction(acc, 1 + i, pbuf[pl.ds(32 * i, 32), :])
    lift = jnp.where(
        (iota((96, 32), 1) >> 3) == (iota((96, 32), 0).astype(F32) * (1.0 / NV) + 1e-3).astype(jnp.int32),
        1.0, 0.0,
    ).astype(F32)
    rows96 = iota((96, 32), 0)
    inner = rows96 - NV * (rows96.astype(F32) * (1.0 / NV) + 1e-3).astype(jnp.int32)
    lift = jnp.where((inner >> 2) == (iota((96, 32), 1) & 7), lift, 0.0)
    spread_p = dot(lift, own_p)
    keep = (iota((96, 128), 0) & 3) == (iota((96, 128), 1) >> 5)
    z = jnp.where(keep, spread_p, 0.0) * (1.0 - MIDDLE_DAMPING * MIDDLE_SHIFT)
    z = z - MIDDLE_DAMPING * jnp.concatenate(acc, axis=0)
    to_sites = jnp.where((li & 31) == (lj >> 2), 1.0, 0.0).astype(F32)
    u = dot(z, to_sites)
    same = jnp.where((li >> 2) == (lj >> 2), MIDDLE_DAMPING, 0.0).astype(F32)
    base = dot(sums, same)

    for copy in copies6:
        copy.wait_recv()
    total = tsend[...]
    for i in range(len(plane)):
        total = total + tbuf[i]
    total = jnp.sum(total, axis=1, keepdims=True)
    t = [total[i : i + 1] for i in range(8)]
    ff, ss, cre, cim, f_re, f_im, s_re, s_im = t
    det = ff * ss - cre * cre - cim * cim
    c1r = (ss * f_re - (cre * s_re - cim * s_im)) / det
    c1i = (ss * f_im - (cre * s_im + cim * s_re)) / det
    c2r = (ff * s_re - (cre * f_re + cim * f_im)) / det
    c2i = (ff * s_im - (cre * f_im - cim * f_re)) / det
    ur_re, ur_im, uf_re, uf_im = (u[NV * q : NV * (q + 1)] for q in range(4))
    up_re = base[:NV] + c1r * ur_re - c1i * ur_im + c2r * uf_re - c2i * uf_im
    up_im = base[NV:] + c1r * ur_im + c1i * ur_re + c2r * uf_im + c2i * uf_re
    up_re = up_re.astype(BF16).astype(F32)
    up_im = up_im.astype(BF16).astype(F32)
    out_re = second_value[:NSC]
    out_im = second_value[NSC:]
    for k in range(NV):
        fre = fine32[pl.ds(k * NSC, NSC), :]
        fim = fine32[pl.ds((NV + k) * NSC, NSC), :]
        a, b = up_re[k : k + 1], up_im[k : k + 1]
        out_re = out_re + fre * a - fim * b
        out_im = out_im + fre * b + fim * a
    solution_ref[...] = jnp.concatenate([out_re, out_im], axis=0)
    for copy in pending:
        copy.wait_send()


def shards(sizes, source_field, gauge_links, fine_vectors, middle_blocks, middle_vectors, bottom_blocks):
    lines, hops, plane, spread, peers = plan(sizes)
    n_xy = sizes[2]
    chunks = n_xy * NV * NV // 128
    width = -(-n_xy * NV // 128) * 128
    copies = 3 * len(hops) + len(spread) + len(lines) - 1 + len(plane)
    vmem = pl.BlockSpec(memory_space=pltpu.VMEM)
    hbm = pl.BlockSpec(memory_space=pl.ANY)
    out = jax.ShapeDtypeStruct((24, 128), F32)
    results = pl.pallas_call(
        functools.partial(kernel, sizes),
        out_shape=(out, out),
        in_specs=[vmem, hbm, vmem, hbm, hbm, hbm],
        out_specs=(vmem, vmem),
        scratch_shapes=[
            pltpu.VMEM((144, 128), F32),
            pltpu.VMEM((2 * 9 * NV * 6, 128), F32),
            pltpu.VMEM((2 * NV * 6, 128), F32),
            pltpu.VMEM(((15 * chunks + 7) // 8 * 8, 128), F32),
            pltpu.VMEM((2 * NV * NSC, 128), F32),
            pltpu.VMEM((192, 128), F32),
            pltpu.VMEM((192, 128), F32),
            pltpu.VMEM((24, 128), F32),
            pltpu.VMEM((width, n_xy * NV * NV), BF16),
            pltpu.VMEM((width, n_xy * NV * NV), BF16),
            pltpu.VMEM((8, width), F32),
            pltpu.VMEM((len(lines) * n_xy, 8, width), F32),
            pltpu.VMEM((8, width), F32),
            pltpu.VMEM((len(lines), 8, width), F32),
            pltpu.VMEM((32, 128), F32),
            pltpu.VMEM((6 * 32, 128), F32),
            pltpu.VMEM((8, width), F32),
            pltpu.VMEM((len(plane), 8, width), F32),
            pltpu.SemaphoreType.DMA((4,)),
            pltpu.SemaphoreType.DMA((copies,)),
            pltpu.SemaphoreType.DMA((copies,)),
        ],
        compiler_params=pltpu.CompilerParams(
            collective_id=0, has_side_effects=True, vmem_limit_bytes=60 * 1024 * 1024
        ),
    )(
        source_field.reshape(24, 128),
        gauge_links.reshape(144, 128),
        fine_vectors.reshape(2 * NV * NSC, 128),
        middle_blocks.reshape(-1, 128),
        middle_vectors.reshape(-1, 128),
        bottom_blocks.reshape(-1, 128),
    )
    return tuple(x.reshape(source_field.shape) for x in results)


def solution(mesh):
    sizes = tuple(mesh.shape[a] for a in AXES)
    return jax.shard_map(
        functools.partial(shards, sizes),
        mesh=mesh,
        in_specs=(
            P(None, None, None, "ta", "gz", "xy", None),
            P(None, None, None, None, "ta", "gz", "xy", None),
            P(None, None, None, None, "ta", "gz", "xy", None),
            P(None, None, None, "ta", "gz", "xy", None),
            P(None, None, "ta", "gz", "xy", None),
            P(None, None, "ta", "gz", None),
        ),
        out_specs=(
            P(None, None, None, "ta", "gz", "xy", None),
            P(None, None, None, "ta", "gz", "xy", None),
        ),
        check_vma=False,
    )
```

profile of v0, /device:TPU:0, one launch (start us, length us, event | category | flops | bytes accessed | tf_op | source)
XLA Modules:
  0.0 35.9 jit_solution(10974683870437201381)
XLA Ops:
  0.6 1.0 %copy.11 = bf16[2,24,4,3,1,1,1,128]{7,3,2,1,0,6,5,4:T(4,128)(2,1)S(1)} copy(bf16[2,24,4,3,1,1,1,128]{7,2,6,5,4,3,1,0:T(4,128)(2,1)} %param.8) | data formatting | bytes 294912 | tf_op args[2]
  1.6 0.8 %reshape.30.fine = bf16[576,128]{1,0:T(8,128)(2,1)} reshape(bf16[2,24,4,3,1,1,1,128]{7,3,2,1,0,6,5,4:T(4,128)(2,1)S(1)} %copy.11) | data formatting | bytes 294912 | tf_op jit(solution)/shard_map/reshape | solution.py:506
  2.4 1.2 %reduce = f32[2,7,2304]{2,1,0:T(8,128)S(1)} reduce(f32[2,7,1,1,2304]{4,3,2,1,0:T(1,128)} %param.11, f32[]{:T(128)} %constant.6), dimensions={2,3}, to_apply=%param.11.reduce_sub_computation | reduce | bytes 258052 | tf_op args[5]
  3.6 0.7 %reshape.33.bb_hbm = f32[252,128]{1,0:T(8,128)} reshape(f32[2,7,2304]{2,1,0:T(8,128)S(1)} %reduce) | data formatting | bytes 258048 | tf_op jit(solution)/shard_map/reshape | solution.py:509
  4.3 28.9 %shard_map.77 = (f32[24,128]{1,0:T(8,128)}, f32[24,128]{1,0:T(8,128)}) custom-call(f32[24,128]{1,0:T(8,128)} %bitcast.11, f32[144,128]{1,0:T(8,128)} %bitcast.10, bf16[576,128]{1,0:T(8,128)(2,1)} %reshape.30.fine, f32[2592,128]{1,0:T(8,128)} %bitcast.8, f32[288,128]{1,0:T(8,128)} %bitcast.9, f32[252,128]{1,0:T(8,128)} %reshape.33.bb_hbm), custom_call_target="tpu_custom_call" | custom-call | tf_op jit(solution)/shard_map/pallas_call | solution.py:472
  33.2 1.3 %copy.16 = f32[2,4,3,1,1,1,128]{6,5,4,3,2,1,0:T(1,128)} copy(f32[2,4,3,1,1,1,128]{6,5,4,3,2,1,0:T(1,128)} %bitcast.13) | data formatting | bytes 24576
  34.5 1.3 %copy.17 = f32[2,4,3,1,1,1,128]{6,5,4,3,2,1,0:T(1,128)} copy(f32[2,4,3,1,1,1,128]{6,5,4,3,2,1,0:T(1,128)} %bitcast.12) | data formatting | bytes 24576
where the time goes:
time: 36.2 us; the launch traced here: 35.9 us
  Pallas kernels  28.9 us (80%)
  local copies, waits for them, and re-layouts  5.05 us (14%)
  other arithmetic  1.21 us (3%)
  between operations  0.65 us (2%)
    pallas_call x1, Pallas kernels, shards(): pl.pallas_call(functools.partial(kernel, sizes), out_shape=(out, out), in...  28.9 us
    unnamed x3, local copies, waits for them, and re-layouts  3.61 us
    unnamed x1, other arithmetic  1.21 us
    reshape x1, local copies, waits for them, and re-layouts, shards(): fine_vectors.reshape(2 * NV * NSC, 128)  0.77 us

commit v1 on v0

--- a/solution.py
+++ b/solution.py
@@ -40,8 +40,12 @@
             hops.append(tuple(offset))
     plane = [(a, b) for a in range(n_ta) for b in range(n_gz) if (a, b) != (0, 0)]
     spread = [(a, b, x) for a, b in lines for x in range(n_xy) if (a, b, x) != (0, 0, 0)]
+    def distance(offset):
+        return sum(min(o, n - o) for o, n in zip(offset, sizes))
+
+    far = [o for o in [(a, b, 0) for a, b in plane] + spread if distance(o) > 3]
     peers = []
-    for offset in hops + [(a, b, 0) for a, b in plane] + spread:
+    for offset in hops + far:
         back = tuple(-o % n for o, n in zip(offset, sizes))
         for one in (offset, back):
             if one not in peers:
@@ -150,9 +154,9 @@
 
 
 def kernel(
-    sizes, source, gauge_hbm, fine, mb_hbm, mv_hbm, bb_hbm,
-    solution_ref, residual_ref,
-    gauge, mb, mv, bb, fine32, near1, near2, second, expand, reduce,
+    sizes, source, gauge_hbm, fine_hbm, mb_hbm, mv_hbm, bb_hbm,
+    result_ref,
+    gauge, fine, mb, mv, bb, fine32, near1, near2, second, expand, reduce,
     rsend, rbuf, fsend, fbuf, psend, pbuf, tsend, tbuf,
     local_sem, send_sem, recv_sem,
 ):
@@ -169,8 +173,10 @@
         pltpu.make_async_copy(gauge_hbm, gauge, local_sem.at[0]),
         pltpu.make_async_copy(mb_hbm, mb, local_sem.at[1]),
         pltpu.make_async_copy(mv_hbm, mv, local_sem.at[2]),
-        pltpu.make_async_copy(bb_hbm, bb.at[pl.ds(0, 14 * chunks)], local_sem.at[3]),
+        pltpu.make_async_copy(bb_hbm.at[:, 0, :], bb.at[pl.ds(0, 14 * chunks)], local_sem.at[3]),
     ]
+    fine_copy = pltpu.make_async_copy(fine_hbm, fine, local_sem.at[4])
+    loads.append(fine_copy)
     barrier = pltpu.get_barrier_semaphore()
     for offset in peers:
         pl.semaphore_signal(barrier, inc=1, device_id=device(offset), device_id_type=MESH)
@@ -215,7 +221,8 @@
     lane = iota((width, cols), 0).astype(F32)
     expand[...] = jnp.where(lane == xs * NV + ks, 1.0, 0.0).astype(BF16)
     reduce[...] = jnp.where(lane == xs * NV + js, 1.0, 0.0).astype(BF16)
-    fine32[...] = fine[...].astype(F32)
+    fine_copy.wait()
+    fine32[...] = fine[...].astype(F32).reshape(2 * NV * NSC, 128)
 
     def loader(buf, scaled):
         def load(spin, color):
@@ -245,7 +252,7 @@
         copy.wait_recv()
     hop = hopping(loader(near2, False), gauge)
     smoothed = src - (twisted(second_value) - 0.5 * hop)
-    residual_ref[...] = smoothed
+    result_ref[pl.ds(24, 24), :] = smoothed
     low = smoothed.astype(BF16).astype(F32)
 
     mre = jnp.zeros((NV, 128), F32)
@@ -253,7 +260,8 @@
     for i in range(NSC):
         fre = fine32[pl.ds(i, NV, stride=NSC), :]
         fim = fine32[pl.ds(NV * NSC + i, NV, stride=NSC), :]
-        rre, rim = low[i : i + 1], low[NSC + i : NSC + i + 1]
+        at = i % 4 * NC + i // 4
+        rre, rim = low[at : at + 1], low[NSC + at : NSC + at + 1]
         mre = mre + fre * rre + fim * rim
         mim = mim + fre * rim - fim * rre
     sums = jnp.concatenate([mre, mim], axis=0)
@@ -447,17 +455,26 @@
     up_im = base[NV:] + c1r * ur_im + c1i * ur_re + c2r * uf_im + c2i * uf_re
     up_re = up_re.astype(BF16).astype(F32)
     up_im = up_im.astype(BF16).astype(F32)
-    out_re = second_value[:NSC]
-    out_im = second_value[NSC:]
+    out_re = jnp.zeros((NSC, 128), F32)
+    out_im = jnp.zeros((NSC, 128), F32)
     for k in range(NV):
         fre = fine32[pl.ds(k * NSC, NSC), :]
         fim = fine32[pl.ds((NV + k) * NSC, NSC), :]
         a, b = up_re[k : k + 1], up_im[k : k + 1]
         out_re = out_re + fre * a - fim * b
         out_im = out_im + fre * b + fim * a
-    solution_ref[...] = jnp.concatenate([out_re, out_im], axis=0)
+    order = [c * 4 + spin for spin in range(4) for c in range(NC)]
+    correction = jnp.concatenate(
+        [part[i : i + 1] for part in (out_re, out_im) for i in order], axis=0
+    )
+    result_ref[pl.ds(0, 24), :] = second_value + correction
     for copy in pending:
         copy.wait_send()
+
+
+def part_outputs(both, solution_ref, residual_ref):
+    solution_ref[...] = both[pl.ds(0, 24), :]
+    residual_ref[...] = both[pl.ds(24, 24), :]
 
 
 def shards(sizes, source_field, gauge_links, fine_vectors, middle_blocks, middle_vectors, bottom_blocks):
@@ -469,13 +486,14 @@
     vmem = pl.BlockSpec(memory_space=pltpu.VMEM)
     hbm = pl.BlockSpec(memory_space=pl.ANY)
     out = jax.ShapeDtypeStruct((24, 128), F32)
-    results = pl.pallas_call(
+    both = pl.pallas_call(
         functools.partial(kernel, sizes),
-        out_shape=(out, out),
-        in_specs=[vmem, hbm, vmem, hbm, hbm, hbm],
-        out_specs=(vmem, vmem),
+        out_shape=jax.ShapeDtypeStruct((48, 128), F32),
+        in_specs=[vmem, hbm, hbm, hbm, hbm, hbm],
+        out_specs=vmem,
         scratch_shapes=[
             pltpu.VMEM((144, 128), F32),
+            pltpu.VMEM((2 * NV * NC, 4, 128), BF16),
             pltpu.VMEM((2 * 9 * NV * 6, 128), F32),
             pltpu.VMEM((2 * NV * 6, 128), F32),
             pltpu.VMEM(((15 * chunks + 7) // 8 * 8, 128), F32),
@@ -493,7 +511,7 @@
             pltpu.VMEM((6 * 32, 128), F32),
             pltpu.VMEM((8, width), F32),
             pltpu.VMEM((len(plane), 8, width), F32),
-            pltpu.SemaphoreType.DMA((4,)),
+            pltpu.SemaphoreType.DMA((5,)),
             pltpu.SemaphoreType.DMA((copies,)),
             pltpu.SemaphoreType.DMA((copies,)),
         ],
@@ -503,11 +521,14 @@
     )(
         source_field.reshape(24, 128),
         gauge_links.reshape(144, 128),
-        fine_vectors.reshape(2 * NV * NSC, 128),
+        jnp.swapaxes(fine_vectors, 2, 3).reshape(2 * NV * NC, 4, 128),
         middle_blocks.reshape(-1, 128),
         middle_vectors.reshape(-1, 128),
-        bottom_blocks.reshape(-1, 128),
-    )
+        bottom_blocks.reshape(-1, 1, 128),
+    )
+    results = pl.pallas_call(
+        part_outputs, out_shape=(out, out), in_specs=[vmem], out_specs=(vmem, vmem)
+    )(both)
     return tuple(x.reshape(source_field.shape) for x in results)
 
 

time: 36.2 us -> 29.5 us (0.81)
  local copies, waits for them, and re-layouts: 5.05 us -> 0 us
  other arithmetic: 1.21 us -> 0 us
    unnamed x3 -> x0, local copies, waits for them, and re-layouts: 3.61 us -> none
    reshape x2 -> x0, local copies, waits for them, and re-layouts: 1.43 us -> none  [the longest x1 0.77 us: shards(): fine_vectors.reshape(2 * NV * NSC, 128)]
    unnamed x1 -> x0, other arithmetic: 1.21 us -> none
    pallas_call x1 -> x2, Pallas kernels: 28.9 us -> 28.6 us  [the longest x1 27.3 us: shards(): pl.pallas_call(functools.partial(kernel, sizes), out_shape=jax.ShapeDtype...]
where the time goes in v1:
time: 29.5 us; the launch traced here: 29.3 us
  Pallas kernels  28.6 us (97%)
  between operations  0.64 us (2%)
    pallas_call x1, Pallas kernels, shards(): pl.pallas_call(functools.partial(kernel, sizes), out_shape=jax.ShapeDtype...  27.3 us
    pallas_call x1, Pallas kernels, shards(): pl.pallas_call(part_outputs, out_shape=(out, out), in_specs=[vmem], out_s...  1.34 us

profile of v1, /device:TPU:0, one launch (start us, length us, event | category | flops | bytes accessed | tf_op | source)
XLA Modules:
  0.0 29.3 jit_solution(15227891089035139643)
XLA Ops:
  0.6 27.3 %shard_map.77.both = f32[48,128]{1,0:T(8,128)} custom-call(f32[24,128]{1,0:T(8,128)} %bitcast.15, f32[144,128]{1,0:T(8,128)} %bitcast.14, bf16[144,4,128]{2,1,0:T(4,128)(2,1)} %bitcast.11, f32[2592,128]{1,0:T(8,128)} %bitcast.10, f32[288,128]{1,0:T(8,128)} %bitcast.12, f32[252,1,128]{2,1,0:T(1,128)} %bitcast.13), custom_call_target="tpu_custom_call" | custom-call | tf_op jit(solution)/shard_map/pallas_call | solution.py:489
  27.9 1.3 %shard_map.78 = (f32[24,128]{1,0:T(8,128)}, f32[24,128]{1,0:T(8,128)}) custom-call(f32[48,128]{1,0:T(8,128)} %shard_map.77.both), custom_call_target="tpu_custom_call" | custom-call | tf_op jit(solution)/shard_map/pallas_call | solution.py:529

commit v2 on v1

--- a/solution.py
+++ b/solution.py
@@ -32,6 +32,12 @@
         reduced = (offset[0] % n_ta, offset[1] % n_gz)
         if reduced not in lines:
             lines.append(reduced)
+    wide = list(lines)
+    for a in lines:
+        for b in lines:
+            both = ((a[0] + b[0]) % n_ta, (a[1] + b[1]) % n_gz)
+            if both not in wide:
+                wide.append(both)
     hops = []
     for axis in range(3):
         for step in (1, -1):
@@ -39,7 +45,7 @@
             offset[axis] = -step % sizes[axis]
             hops.append(tuple(offset))
     plane = [(a, b) for a in range(n_ta) for b in range(n_gz) if (a, b) != (0, 0)]
-    spread = [(a, b, x) for a, b in lines for x in range(n_xy) if (a, b, x) != (0, 0, 0)]
+    spread = [(a, b, x) for a, b in wide for x in range(n_xy) if (a, b, x) != (0, 0, 0)]
     def distance(offset):
         return sum(min(o, n - o) for o, n in zip(offset, sizes))
 
@@ -50,7 +56,7 @@
         for one in (offset, back):
             if one not in peers:
                 peers.append(one)
-    return lines, hops, plane, spread, peers
+    return lines, wide, hops, plane, spread, peers
 
 
 def dot(a, b, dims=((1,), (0,))):
@@ -154,14 +160,14 @@
 
 
 def kernel(
-    sizes, source, gauge_hbm, fine_hbm, mb_hbm, mv_hbm, bb_hbm,
+    sizes, source_hbm, gauge_hbm, fine_hbm, mb_hbm, mv_hbm, bb_hbm,
     result_ref,
-    gauge, fine, mb, mv, bb, fine32, near1, near2, second, expand, reduce,
-    rsend, rbuf, fsend, fbuf, psend, pbuf, tsend, tbuf,
+    source, gauge, fine, mb, mv, bb, fine32, near1, near2, second, expand, reduce,
+    rsend, rbuf, psend, pbuf, tsend, tbuf,
     local_sem, send_sem, recv_sem,
 ):
     n_ta, n_gz, n_xy = sizes
-    lines, hops, plane, spread, peers = plan(sizes)
+    lines, wide, hops, plane, spread, peers = plan(sizes)
     me = tuple(lax.axis_index(a) for a in AXES)
     chunks = n_xy * NV * NV // 128
     width = rsend.shape[1]
@@ -173,19 +179,21 @@
         pltpu.make_async_copy(gauge_hbm, gauge, local_sem.at[0]),
         pltpu.make_async_copy(mb_hbm, mb, local_sem.at[1]),
         pltpu.make_async_copy(mv_hbm, mv, local_sem.at[2]),
-        pltpu.make_async_copy(bb_hbm.at[:, 0, :], bb.at[pl.ds(0, 14 * chunks)], local_sem.at[3]),
+        pltpu.make_async_copy(bb_hbm.at[:, 0, :], bb.at[0, pl.ds(0, 14 * chunks)], local_sem.at[3]),
     ]
     fine_copy = pltpu.make_async_copy(fine_hbm, fine, local_sem.at[4])
-    loads.append(fine_copy)
+    source_copy = pltpu.make_async_copy(source_hbm, source, local_sem.at[5])
+    loads = [source_copy, loads[0], loads[3], loads[2], loads[1], fine_copy]
     barrier = pltpu.get_barrier_semaphore()
     for offset in peers:
         pl.semaphore_signal(barrier, inc=1, device_id=device(offset), device_id_type=MESH)
     for load in loads:
         load.start()
 
-    bb[pl.ds(14 * chunks, bb.shape[0] - 14 * chunks), :] = jnp.zeros(
-        (bb.shape[0] - 14 * chunks, 128), F32
-    )
+    for i in range(len(lines)):
+        bb[i, pl.ds(14 * chunks, bb.shape[1] - 14 * chunks), :] = jnp.zeros(
+            (bb.shape[1] - 14 * chunks, 128), F32
+        )
     count = [0]
 
     def send(src, dst, offset):
@@ -197,6 +205,7 @@
         copy.start()
         return copy
 
+    source_copy.wait()
     pl.semaphore_wait(barrier, len(peers))
     pending = []
 
@@ -209,6 +218,19 @@
 
     copies1 = halo(source, near1)
     pending += copies1
+    loads[2].wait()
+
+    def bulk(first_line, last_line):
+        return [
+            send(
+                bb.at[0, pl.ds(0, 14 * chunks)],
+                bb.at[lines.index((-a % n_ta, -b % n_gz)), pl.ds(0, 14 * chunks)],
+                (a, b, 0),
+            )
+            for a, b in lines[first_line:last_line]
+        ]
+
+    bulks = bulk(1, 2)
     src = source[...]
     fill_y(src, near1)
     first = FINE_DAMPING * precondition(src)
@@ -236,7 +258,7 @@
             return a * re + b * im, a * im - b * re
         return load
 
-    loads[0].wait()
+    loads[1].wait()
     for copy in copies1:
         copy.wait_recv()
     hop = hopping(loader(near1, True), gauge)
@@ -244,10 +266,11 @@
     second[...] = second_value
     copies2 = halo(second, near2)
     pending += copies2
+    bulks += bulk(2, len(lines))
+    pending += bulks
     fill_y(second_value, near2)
-    loads[2].wait()
     loads[3].wait()
-    loads[1].wait()
+    loads[4].wait()
     for copy in copies2:
         copy.wait_recv()
     hop = hopping(loader(near2, False), gauge)
@@ -296,7 +319,7 @@
     rsend[...] = own_tile
     copies3 = []
     for a, b, x in spread:
-        slot = lines.index((-a % n_ta, -b % n_gz))
+        slot = wide.index((-a % n_ta, -b % n_gz))
         copies3.append(send(rsend, rbuf.at[slot * n_xy + x], (a, b, x)))
     pending += copies3
 
@@ -318,7 +341,7 @@
         copy.wait_recv()
 
     def line_slot(offset):
-        return lines.index((offset[0] % n_ta, offset[1] % n_gz))
+        return wide.index((offset[0] % n_ta, offset[1] % n_gz))
 
     near_offsets = ((1, 0), (-1, 0), (0, 1), (0, -1))
     length = n_xy * NV
@@ -333,25 +356,32 @@
             one, two = pltpu.roll(v, -shift, 1), pltpu.roll(v, width - (length + shift), 1)
         return jnp.where(lanes < length, jnp.where(inside, one, two), 0.0)
 
-    def bottom(own, others):
-        near = [own] + others + [turn(own, NV), turn(own, -NV)]
+    def bottom(systems):
         zero = jnp.zeros((1, width), F32)
-        stack = jnp.concatenate(
-            [v[0:1] for v in near] + [zero] + [v[1:2] for v in near] + [zero], axis=0
-        )
-        wide = split_dot(stack, expand[...], ((1,), (0,)))
-        parts = []
-        for c in range(chunks):
-            bre = bb[pl.ds(c, 8, stride=chunks), :]
-            bim = bb[pl.ds(7 * chunks + c, 8, stride=chunks), :]
-            vre = wide[0:8, c * 128 : (c + 1) * 128]
-            vim = wide[8:16, c * 128 : (c + 1) * 128]
-            parts.append(jnp.concatenate([bre * vre - bim * vim, bre * vim + bim * vre], axis=0))
-        prod = jnp.concatenate(parts, axis=1)
-        short = split_dot(prod, reduce[...], ((1,), (1,)))
-        re = jnp.sum(short[0:8], axis=0, keepdims=True)
-        im = jnp.sum(short[8:16], axis=0, keepdims=True)
-        return pair_tile(re, im) + BOTTOM_SHIFT * own
+        stacks = []
+        for own, others, _ in systems:
+            near = [own] + others + [turn(own, NV), turn(own, -NV)]
+            stacks += [v[0:1] for v in near] + [zero] + [v[1:2] for v in near] + [zero]
+        broad = split_dot(jnp.concatenate(stacks, axis=0), expand[...], ((1,), (0,)))
+        prods = []
+        for q, (_, _, line) in enumerate(systems):
+            parts = []
+            for c in range(chunks):
+                bre = bb[line, pl.ds(c, 8, stride=chunks), :]
+                bim = bb[line, pl.ds(7 * chunks + c, 8, stride=chunks), :]
+                vre = broad[16 * q : 16 * q + 8, c * 128 : (c + 1) * 128]
+                vim = broad[16 * q + 8 : 16 * q + 16, c * 128 : (c + 1) * 128]
+                parts.append(
+                    jnp.concatenate([bre * vre - bim * vim, bre * vim + bim * vre], axis=0)
+                )
+            prods.append(jnp.concatenate(parts, axis=1))
+        short = split_dot(jnp.concatenate(prods, axis=0), reduce[...], ((1,), (1,)))
+        results = []
+        for q, (own, _, _) in enumerate(systems):
+            re = jnp.sum(short[16 * q : 16 * q + 8], axis=0, keepdims=True)
+            im = jnp.sum(short[16 * q + 8 : 16 * q + 16], axis=0, keepdims=True)
+            results.append(pair_tile(re, im) + BOTTOM_SHIFT * own)
+        return results
 
     def gathered(slot):
         total = own_tile if slot == 0 else rbuf[slot * n_xy]
@@ -359,23 +389,21 @@
             total = total + rbuf[slot * n_xy + x]
         return total
 
-    slots = [gathered(s) for s in range(len(lines))]
+    slots = [gathered(s) for s in range(len(wide))]
     r = slots[0]
-    f = bottom(r, [slots[line_slot(o)] for o in near_offsets])
-    fsend[...] = f
-    copies4 = []
+    for copy in bulks:
+        copy.wait_recv()
+    systems = []
     for i, (a, b) in enumerate(lines):
-        if i:
-            copies4.append(send(fsend, fbuf.at[lines.index((-a % n_ta, -b % n_gz))], (a, b, 0)))
-    pending += copies4
+        systems.append((slots[i], [slots[line_slot((a + p, b + q))] for p, q in near_offsets], i))
+    images = bottom(systems)
+    f = images[0]
     fcol_re = jnp.sum(jnp.where(place, f[0:1], 0.0), axis=1, keepdims=True)
     fcol_im = jnp.sum(jnp.where(place, f[1:2], 0.0), axis=1, keepdims=True)
     psend[pl.ds(16, 16), :] = prolong(fcol_re, fcol_im)
     copies5 = [send(psend, pbuf.at[pl.ds(32 * i, 32)], offset) for i, offset in enumerate(hops)]
     pending += copies5
-    for copy in copies4:
-        copy.wait_recv()
-    s = bottom(f, [fbuf[line_slot(o)] for o in near_offsets])
+    s = bottom([(f, [images[line_slot(o)] for o in near_offsets], 0)])[0]
 
     rr, ri, fr, fi, sr, si = r[0:1], r[1:2], f[0:1], f[1:2], s[0:1], s[1:2]
     tsend[...] = jnp.concatenate(
@@ -478,7 +506,7 @@
 
 
 def shards(sizes, source_field, gauge_links, fine_vectors, middle_blocks, middle_vectors, bottom_blocks):
-    lines, hops, plane, spread, peers = plan(sizes)
+    lines, wide, hops, plane, spread, peers = plan(sizes)
     n_xy = sizes[2]
     chunks = n_xy * NV * NV // 128
     width = -(-n_xy * NV // 128) * 128
@@ -489,14 +517,15 @@
     both = pl.pallas_call(
         functools.partial(kernel, sizes),
         out_shape=jax.ShapeDtypeStruct((48, 128), F32),
-        in_specs=[vmem, hbm, hbm, hbm, hbm, hbm],
+        in_specs=[hbm] * 6,
         out_specs=vmem,
         scratch_shapes=[
+            pltpu.VMEM((24, 128), F32),
             pltpu.VMEM((144, 128), F32),
             pltpu.VMEM((2 * NV * NC, 4, 128), BF16),
             pltpu.VMEM((2 * 9 * NV * 6, 128), F32),
             pltpu.VMEM((2 * NV * 6, 128), F32),
-            pltpu.VMEM(((15 * chunks + 7) // 8 * 8, 128), F32),
+            pltpu.VMEM((len(lines), (15 * chunks + 7) // 8 * 8, 128), F32),
             pltpu.VMEM((2 * NV * NSC, 128), F32),
             pltpu.VMEM((192, 128), F32),
             pltpu.VMEM((192, 128), F32),
@@ -504,14 +533,12 @@
             pltpu.VMEM((width, n_xy * NV * NV), BF16),
             pltpu.VMEM((width, n_xy * NV * NV), BF16),
             pltpu.VMEM((8, width), F32),
-            pltpu.VMEM((len(lines) * n_xy, 8, width), F32),
-            pltpu.VMEM((8, width), F32),
-            pltpu.VMEM((len(lines), 8, width), F32),
+            pltpu.VMEM((len(wide) * n_xy, 8, width), F32),
             pltpu.VMEM((32, 128), F32),
             pltpu.VMEM((6 * 32, 128), F32),
             pltpu.VMEM((8, width), F32),
             pltpu.VMEM((len(plane), 8, width), F32),
-            pltpu.SemaphoreType.DMA((5,)),
+            pltpu.SemaphoreType.DMA((6,)),
             pltpu.SemaphoreType.DMA((copies,)),
             pltpu.SemaphoreType.DMA((copies,)),
         ],

time: 29.5 us -> 28.3 us (0.959)
  Pallas kernels: 28.6 us -> 27.4 us
    pallas_call x1, Pallas kernels: 27.3 us -> 26.1 us  [shards(): pl.pallas_call(functools.partial(kernel, sizes), out_shape=jax.ShapeDtype...]
where the time goes in v2:
time: 28.3 us; the launch traced here: 28.1 us
  Pallas kernels  27.4 us (97%)
  between operations  0.64 us (2%)
    pallas_call x1, Pallas kernels, shards(): pl.pallas_call(functools.partial(kernel, sizes), out_shape=jax.ShapeDtype...  26.1 us
    pallas_call x1, Pallas kernels, shards(): pl.pallas_call(part_outputs, out_shape=(out, out), in_specs=[vmem], out_s...  1.34 us

profile of v2, /device:TPU:0, one launch (start us, length us, event | category | flops | bytes accessed | tf_op | source)
XLA Modules:
  0.0 28.1 jit_solution(3953485206290215271)
XLA Ops:
  0.6 26.1 %shard_map.77.both = f32[48,128]{1,0:T(8,128)} custom-call(f32[24,128]{1,0:T(8,128)} %bitcast.15, f32[144,128]{1,0:T(8,128)} %bitcast.14, bf16[144,4,128]{2,1,0:T(4,128)(2,1)} %bitcast.11, f32[2592,128]{1,0:T(8,128)} %bitcast.10, f32[288,128]{1,0:T(8,128)} %bitcast.12, f32[252,1,128]{2,1,0:T(1,128)} %bitcast.13), custom_call_target="tpu_custom_call" | custom-call | tf_op jit(solution)/shard_map/pallas_call | solution.py:517
  26.7 1.3 %shard_map.78 = (f32[24,128]{1,0:T(8,128)}, f32[24,128]{1,0:T(8,128)}) custom-call(f32[48,128]{1,0:T(8,128)} %shard_map.77.both), custom_call_target="tpu_custom_call" | custom-call | tf_op jit(solution)/shard_map/pallas_call | solution.py:556
